TPU v7x, 32 devices: a whole 2x2x4 slice. The times are simulated.
32 devices in a mesh: dp: 8 (over z, x), txt: 4 (over y, core).
Axes of the slice: x: 2, y: 2, z: 4, core: 2. Of those that a mesh axis runs over, the one named last changes fastest.
Arguments:
- resid: bfloat16 [2048, 1024], P('dp', 'txt'), may hold values from -40 to 40
- prenorm_gain: float32 [1024], replicated, may hold values from 0.25 to 1.75
- prenorm_bias: float32 [1024], replicated, may hold values from -3 to 3
- up_weight: bfloat16 [1024, 4096], P('dp', 'txt'), may hold values from -0.1875 to 0.1875
- up_bias: float32 [4096], P('txt'), may hold values from -3 to 3
- down_weight: bfloat16 [4096, 1024], P('txt', 'dp'), may hold values from -0.09375 to 0.09375
- down_bias: float32 [1024], replicated, may hold values from -3 to 3
- post_gain: float32 [1024], P('txt'), may hold values from 0.25 to 1.75
- post_bias: float32 [1024], P('txt'), may hold values from -3 to 3
- projection: bfloat16 [1024, 768], P('txt'), may hold values from -1 to 1
- texts: bfloat16 [5120, 768], P('txt'), may hold values from -48 to 48
- labels: int32 [2048], P('dp'), may hold values from 0 to 5119
- step_size: float32 [1], replicated, may hold values from 0.5 to 2
Outputs:
- adversarial: float32 [2048, 1024], P('dp', 'txt')
All inputs are finite; a program needn't handle non-finite values.
Results may differ from a plain program's by a relative error of at most 0.0036.
Values may be sent and summed in bfloat16 or wider, within the bound.
A program may use at most 64 MiB of HBM per device.

v0:
```python
import jax
import jax.numpy as jnp
from jax import lax
from jax.sharding import PartitionSpec as P

MODEL_WIDTH = 1024


def local(
    resid,
    prenorm_gain,
    prenorm_bias,
    up_weight,
    up_bias,
    down_weight,
    down_bias,
    post_gain,
    post_bias,
    projection,
    texts,
    labels,
    step_size,
):
    feature_width = resid.shape[1]
    shift_amount = lax.axis_index("txt") * feature_width
    gathered = lax.all_gather(resid, "txt", axis=1, tiled=True)
    input_rows = gathered.astype(jnp.float32)
    input_mean = jnp.mean(input_rows, axis=1, keepdims=True)
    var_in = jnp.mean(input_rows * input_rows, axis=1, keepdims=True) - input_mean * input_mean
    input_inverse_deviation = lax.rsqrt(var_in + 1e-05)
    centered_input = (input_rows - input_mean) * input_inverse_deviation
    normed_input = (centered_input * prenorm_gain + prenorm_bias).astype(jnp.bfloat16)
    w_up = lax.all_gather(up_weight, "dp", axis=0, tiled=True)
    w_down = lax.all_gather(down_weight, "dp", axis=1, tiled=True)
    pre_act = jnp.dot(normed_input, w_up, preferred_element_type=jnp.float32) + up_bias
    gate_sig = jax.nn.sigmoid(1.702 * pre_act)
    hidden = (pre_act * gate_sig).astype(jnp.bfloat16)
    mixed_part = jnp.dot(hidden, w_down, preferred_element_type=jnp.float32)
    mixed = lax.psum_scatter(mixed_part, "txt", scatter_dimension=1, tiled=True)
    own_rows = resid.astype(jnp.float32)
    block_out = own_rows + mixed + lax.dynamic_slice_in_dim(down_bias, shift_amount, feature_width)
    out_sums = lax.psum((jnp.sum(block_out, axis=1), jnp.sum(block_out * block_out, axis=1)), "txt")
    mean_out = out_sums[0][:, None] / MODEL_WIDTH
    var_out = out_sums[1][:, None] / MODEL_WIDTH - mean_out * mean_out
    rstd_out = lax.rsqrt(var_out + 1e-05)
    yhat = (block_out - mean_out) * rstd_out
    post_normed = (yhat * post_gain + post_bias).astype(jnp.bfloat16)
    emb_part = jnp.dot(post_normed, projection, preferred_element_type=jnp.float32)
    embedding = lax.psum_scatter(emb_part, "txt", scatter_dimension=0, tiled=True)
    emb_norm = jnp.sqrt(jnp.sum(embedding * embedding, axis=1, keepdims=True) + 1e-06)
    unit_vec = embedding / emb_norm
    unit_low = lax.all_gather(unit_vec.astype(jnp.bfloat16), "txt", axis=0, tiled=True)
    text_f = texts.astype(jnp.float32)
    text_unit = (text_f / jnp.sqrt(jnp.sum(text_f * text_f, axis=1, keepdims=True) + 1e-06)).astype(
        jnp.bfloat16
    )
    logits = 100.0 * jnp.einsum(
        "ie,je->ij", unit_low, text_unit, preferred_element_type=jnp.float32
    )
    local_top = jnp.max(logits, axis=1)
    row_top = lax.pmax(local_top, "txt")
    exponent = jnp.exp(logits - row_top[:, None])
    row_total = lax.psum(jnp.sum(exponent, axis=1), "txt")
    prob = exponent / row_total[:, None]
    local_label = labels - lax.axis_index("txt") * texts.shape[0]
    columns = lax.broadcasted_iota(jnp.int32, logits.shape, 1)
    target = (columns == local_label[:, None]).astype(jnp.float32)
    score_grad = (100.0 * (prob - target)).astype(jnp.bfloat16)
    back_part = jnp.dot(score_grad, text_unit, preferred_element_type=jnp.float32)
    unit_grad = lax.psum_scatter(back_part, "txt", scatter_dimension=0, tiled=True)
    along = jnp.sum(unit_vec * unit_grad, axis=1, keepdims=True)
    grad_share = ((unit_grad - unit_vec * along) / emb_norm).astype(jnp.bfloat16)
    emb_grad = lax.all_gather(grad_share, "txt", axis=0, tiled=True)
    post_grad = jnp.einsum("ie,de->id", emb_grad, projection, preferred_element_type=jnp.float32)
    scaled = post_grad * post_gain
    back_sums = lax.psum((jnp.sum(scaled, axis=1), jnp.sum(scaled * yhat, axis=1)), "txt")
    output_gradient = (
        scaled - back_sums[0][:, None] / MODEL_WIDTH - yhat * (back_sums[1][:, None] / MODEL_WIDTH)
    ) * rstd_out
    out_full = lax.all_gather(output_gradient.astype(jnp.bfloat16), "txt", axis=1, tiled=True)
    hid_grad = jnp.einsum("id,fd->if", out_full, w_down, preferred_element_type=jnp.float32)
    act_grad = (hid_grad * (gate_sig + 1.702 * pre_act * gate_sig * (1.0 - gate_sig))).astype(
        jnp.bfloat16
    )
    normed_part = jnp.einsum("if,df->id", act_grad, w_up, preferred_element_type=jnp.float32)
    normed_gradient = lax.psum_scatter(normed_part, "txt", scatter_dimension=1, tiled=True)
    centered_input_portion = lax.dynamic_slice_in_dim(
        centered_input, shift_amount, feature_width, 1
    )
    scaled_input = normed_gradient * lax.dynamic_slice_in_dim(
        prenorm_gain, shift_amount, feature_width
    )
    input_row_sums = lax.psum(
        (jnp.sum(scaled_input, axis=1), jnp.sum(scaled_input * centered_input_portion, axis=1)),
        "txt",
    )
    input_gradient = (
        output_gradient
        + (
            scaled_input
            - input_row_sums[0][:, None] / MODEL_WIDTH
            - centered_input_portion * (input_row_sums[1][:, None] / MODEL_WIDTH)
        )
        * input_inverse_deviation
    )
    square_sum = lax.psum(jnp.sum(input_gradient * input_gradient, axis=1), "txt")
    grad_rms = jnp.sqrt(square_sum[:, None] / MODEL_WIDTH + 1e-06)
    return own_rows + step_size[0] * input_gradient / grad_rms


def solution(mesh):
    placed = (
        P("dp", "txt"),
        P(),
        P(),
        P("dp", "txt"),
        P("txt"),
        P("txt", "dp"),
        P(),
        P("txt"),
        P("txt"),
        P("txt", None),
        P("txt", None),
        P("dp"),
        P(),
    )
    return jax.shard_map(
        local, mesh=mesh, in_specs=placed, out_specs=P("dp", "txt"), check_vma=False
    )
```

profile of v0, /device:TPU:0, one launch (start us, length us, event | category | flops | bytes accessed | tf_op | source)
XLA Modules:
  0.0 297.3 jit_solution(12234471146780298693)
XLA Ops:
  8.1 8.9 %all_gather.18 = bf16[256,1024]{1,0:T(8,128)(2,1)S(1)} all-gather(bf16[256,256]{1,0:T(8,128)(2,1)} %param.13), channel_id=1, replica_groups=mesh['dp'=8,'txt'=4] {'txt'}, dimensions={1}, use_global_device_ids=true | all-gather | bytes 655360 | tf_op jit(solution)/shard_map/all_gather | solution.py:26
  17.2 44.1 %all-gather.3.cloned.1.call-done = bf16[1024,1024]{1,0:T(8,128)(2,1)} async-done(((bf16[128,1024]{1,0:T(8,128)(2,1)}), bf16[1024,1024]{1,0:T(8,128)(2,1)}) %all-gather.3.cloned.1.call-update) | async-done | bytes 2097168 | tf_op jit(solution)/shard_map/all_gather | solution.py:33
  61.3 2.4 convolution_add_fusion
  63.7 48.5 %all-gather.5.cloned.1.call-done = bf16[1024,1024]{1,0:T(8,128)(2,1)} async-done(((bf16[1024,128]{1,0:T(8,128)(2,1)}), bf16[1024,1024]{1,0:T(8,128)(2,1)}) %all-gather.5.cloned.1.call-update) | async-done | bytes 2097168 | tf_op jit(solution)/shard_map/all_gather | solution.py:34
  112.3 3.3 %fusion.17 = f32[256,1024]{1,0:T(8,128)} fusion(bf16[1024,1024]{1,0:T(8,128)(2,1)} %all-gather.5.cloned.1.call-done, f32[256,1024]{1,0:T(8,128)S(1)} %convolution_add_fusion), kind=kOutput, calls=%fused_computation.32 | convolution fusion | flops 538443776 | bytes 4194304 | tf_op jit(solution)/shard_map/dot_general | solution.py:38
  115.7 0.9 dynamic_slice.9
  116.6 22.2 %reduce-scatter.5.cloned.1.call-done = f32[256,256]{1,0:T(8,128)} async-done(((f32[256,1024]{1,0:T(8,128)}), f32[256,256]{1,0:T(8,128)}) %reduce-scatter.5.cloned.1.call-update) | async-done | bytes 262160 | tf_op jit(solution)/shard_map/reduce_scatter | solution.py:39
  138.7 1.1 fusion.38
  139.8 5.8 %all-reduce.2 = (f32[256]{0:T(256)S(1)}, f32[256]{0:T(256)S(1)}) all-reduce(f32[256]{0:T(256)S(1)} %get-tuple-element.12, f32[256]{0:T(256)S(1)} %get-tuple-element.11), channel_id=1, replica_groups=mesh['dp'=8,'txt'=4] {'txt'}, use_global_device_ids=true, to_apply=%region_6.0 | all-reduce | flops 512 | bytes 4096 | tf_op jit(solution)/shard_map/psum | solution.py:42
  145.6 1.2 fusion.25
  147.4 1.7 fusion.1
  149.2 21.7 %reduce-scatter.7.cloned.1.call-done = f32[64,768]{1,0:T(8,128)} async-done(((f32[256,768]{1,0:T(8,128)}), f32[64,768]{1,0:T(8,128)}) %reduce-scatter.7.cloned.1.call-update) | async-done | bytes 196624 | tf_op jit(solution)/shard_map/reduce_scatter | solution.py:49
  170.9 1.0 multiply_reduce_fusion.6
  171.9 1.0 fusion.35
  173.0 6.1 %all_gather.21 = bf16[256,768]{1,0:T(8,128)(2,1)S(1)} all-gather(bf16[64,768]{1,0:T(8,128)(2,1)S(1)} %fusion.35), channel_id=1, replica_groups=mesh['dp'=8,'txt'=4] {'txt'}, dimensions={0}, use_global_device_ids=true | all-gather | bytes 491520 | tf_op jit(solution)/shard_map/all_gather | solution.py:52
  179.1 3.5 %fusion.41 = (f32[256]{0:T(256)S(1)}, f32[256,1280]{1,0:T(8,128)}) fusion(bf16[256,768]{1,0:T(8,128)(2,1)S(1)} %all_gather.21, bf16[1280,768]{1,0:T(8,128)(2,1)} %fusion.1), kind=kOutput, calls=%fused_computation.81 | convolution fusion | flops 503971584 | bytes 3671040 | tf_op jit(solution)/shard_map/ie,je->ij/dot_general | solution.py:57
  182.6 6.4 %pmax.7 = f32[256]{0:T(256)S(1)} all-reduce(f32[256]{0:T(256)S(1)} %get-tuple-element.28), channel_id=1, replica_groups=mesh['dp'=8,'txt'=4] {'txt'}, use_global_device_ids=true, to_apply=%region_11.0 | all-reduce | flops 256 | bytes 2048 | tf_op jit(solution)/shard_map/pmax | solution.py:61
  189.0 1.6 fusion.3
  190.7 5.7 %psum.58 = f32[256]{0:T(256)S(1)} all-reduce(f32[256]{0:T(256)S(1)} %fusion.3), channel_id=1, replica_groups=mesh['dp'=8,'txt'=4] {'txt'}, use_global_device_ids=true, to_apply=%region_13.0 | all-reduce | flops 256 | bytes 2048 | tf_op jit(solution)/shard_map/psum | solution.py:63
  196.3 3.2 %fusion.12 = f32[256,768]{1,0:T(8,128)} fusion(bf16[1280,768]{1,0:T(8,128)(2,1)S(1)} %copy-done.2, f32[256,1280]{1,0:T(8,128)} %get-tuple-element.29, s32[256]{0:T(256)S(1)} %broadcast_subtract_fusion, f32[256]{0:T(256)S(1)} %psum.58, f32[256]{0:T(256)S(1)} %pmax.7), kind=kOutput, calls=%fused_computation.27 | convolution fusion | flops 505610240 | bytes 4066304 | tf_op jit(solution)/shard_map/dot_general | solution.py:69
  199.6 23.9 %reduce-scatter.9.cloned.1.call-done = f32[64,768]{1,0:T(8,128)} async-done(((f32[256,768]{1,0:T(8,128)}), f32[64,768]{1,0:T(8,128)}) %reduce-scatter.9.cloned.1.call-update) | async-done | bytes 196624 | tf_op jit(solution)/shard_map/reduce_scatter | solution.py:70
  223.5 1.1 multiply_reduce_fusion.5
  224.6 1.1 divide_convert_fusion
  225.8 6.1 %all_gather.22 = bf16[256,768]{1,0:T(8,128)(2,1)S(1)} all-gather(bf16[64,768]{1,0:T(8,128)(2,1)S(1)} %divide_convert_fusion), channel_id=1, replica_groups=mesh['dp'=8,'txt'=4] {'txt'}, dimensions={0}, use_global_device_ids=true | all-gather | bytes 491520 | tf_op jit(solution)/shard_map/all_gather | solution.py:73
  232.3 6.5 %all-reduce.1 = (f32[256]{0:T(256)S(1)}, f32[256]{0:T(256)S(1)}) all-reduce(f32[256]{0:T(256)S(1)} %get-tuple-element.10, f32[256]{0:T(256)S(1)} %get-tuple-element.9), channel_id=1, replica_groups=mesh['dp'=8,'txt'=4] {'txt'}, use_global_device_ids=true, to_apply=%region_19.0 | all-reduce | flops 512 | bytes 4096 | tf_op jit(solution)/shard_map/psum | solution.py:76
  239.0 6.9 %all_gather.23 = bf16[256,1024]{1,0:T(8,128)(2,1)S(1)} all-gather(bf16[256,256]{1,0:T(8,128)(2,1)S(1)} %get-tuple-element.21), channel_id=1, replica_groups=mesh['dp'=8,'txt'=4] {'txt'}, dimensions={1}, use_global_device_ids=true | all-gather | bytes 655360 | tf_op jit(solution)/shard_map/all_gather | solution.py:80
  245.9 4.7 %fusion.4 = f32[256,1024]{1,0:T(8,128)} fusion(bf16[1024,1024]{1,0:T(8,128)(2,1)} %all-gather.3.cloned.1.call-done, bf16[256,1024]{1,0:T(8,128)(2,1)S(1)} %all_gather.23, bf16[1024,1024]{1,0:T(8,128)(2,1)} %all-gather.5.cloned.1.call-done, f32[256,1024]{1,0:T(8,128)S(1)} %copy-done.9), kind=kOutput, calls=%fused_computation.16 | convolution fusion | flops 1076363264 | bytes 6815744 | tf_op jit(solution)/shard_map/if,df->id/dot_general | solution.py:85
  252.3 23.6 %reduce-scatter.11.cloned.1.call-done = f32[256,256]{1,0:T(8,128)} async-done(((f32[256,1024]{1,0:T(8,128)}), f32[256,256]{1,0:T(8,128)}) %reduce-scatter.11.cloned.1.call-update) | async-done | bytes 262160 | tf_op jit(solution)/shard_map/reduce_scatter | solution.py:86
  275.8 1.1 multiply_reduce_fusion.4
  276.9 5.8 %all-reduce = (f32[256]{0:T(256)S(1)}, f32[256]{0:T(256)S(1)}) all-reduce(f32[256]{0:T(256)S(1)} %get-tuple-element.8, f32[256]{0:T(256)S(1)} %get-tuple-element.7), channel_id=1, replica_groups=mesh['dp'=8,'txt'=4] {'txt'}, use_global_device_ids=true, to_apply=%region_24.0 | all-reduce | flops 512 | bytes 4096 | tf_op jit(solution)/shard_map/psum | solution.py:93
  282.7 1.2 multiply_reduce_fusion
  283.9 5.7 %psum.63 = f32[256]{0:T(256)S(1)} all-reduce(f32[256]{0:T(256)S(1)} %get-tuple-element.19), channel_id=1, replica_groups=mesh['dp'=8,'txt'=4] {'txt'}, use_global_device_ids=true, to_apply=%region_26.0 | all-reduce | flops 256 | bytes 2048 | tf_op jit(solution)/shard_map/psum | solution.py:106
  (48 shorter events, 4.9 us)
Async XLA Ops:
  6.5 139.1 %copy-start = (bf16[256,768]{1,0:T(8,128)(2,1)S(1)}, bf16[256,768]{1,0:T(8,128)(2,1)}, u32[]{:S(2)}) copy-start(bf16[256,768]{1,0:T(8,128)(2,1)} %param.22) | copy-start | bytes 1179652
  6.5 54.8 %all-gather.3.cloned.1.call-start = ((), (), s32[]{:S(2)}) async-start(), calls=%async_computation.4 | async-start | bytes 2359296 | tf_op jit(solution)/shard_map/all_gather | solution.py:33
  7.3 105.0 %all-gather.5.cloned.1.call-start = ((), (), s32[]{:S(2)}) async-start(), calls=%async_computation.5 | async-start | bytes 2359296 | tf_op jit(solution)/shard_map/all_gather | solution.py:34
  8.0 130.7 %reduce-scatter.5.cloned.1.call-start = ((), (), s32[]{:S(2)}) async-start(), calls=%async_computation.6 | async-start | bytes 1310720 | tf_op jit(solution)/shard_map/reduce_scatter | solution.py:39
  63.7 51.9 %copy-start.8 = (f32[256,1024]{1,0:T(8,128)}, f32[256,1024]{1,0:T(8,128)S(1)}, u32[]{:S(2)}) copy-start(f32[256,1024]{1,0:T(8,128)S(1)} %convolution_add_fusion) | copy-start | bytes 3145732
  63.7 75.0 %copy-start.4 = (bf16[256,256]{1,0:T(8,128)(2,1)S(1)}, bf16[256,256]{1,0:T(8,128)(2,1)}, u32[]{:S(2)}) copy-start(bf16[256,256]{1,0:T(8,128)(2,1)} %param.13) | copy-start | bytes 393220
  63.7 81.9 %copy-start.5 = (f32[256]{0:T(256)S(1)}, f32[256]{0:T(256)}, u32[]{:S(2)}) copy-start(f32[256]{0:T(256)} %param.20) | copy-start | bytes 3076
  63.7 81.9 %copy-start.7 = (f32[256]{0:T(256)S(1)}, f32[256]{0:T(256)}, u32[]{:S(2)}) copy-start(f32[256]{0:T(256)} %param.21) | copy-start | bytes 3076
  115.6 31.4 %copy-start.6 = (s32[256]{0:T(256)S(1)}, s32[256]{0:T(256)}, u32[]{:S(2)}) copy-start(s32[256]{0:T(256)} %param.24) | copy-start | bytes 3076
  115.6 31.4 %copy-start.1 = (bf16[1280,768]{1,0:T(8,128)(2,1)S(1)}, bf16[1280,768]{1,0:T(8,128)(2,1)}, u32[]{:S(2)}) copy-start(bf16[1280,768]{1,0:T(8,128)(2,1)} %param.23) | copy-start | bytes 5898244
  115.6 55.3 %reduce-scatter.7.cloned.1.call-start = ((), (), s32[]{:S(2)}) async-start(), calls=%async_computation.7 | async-start | bytes 983040 | tf_op jit(solution)/shard_map/reduce_scatter | solution.py:49
  146.9 76.6 %reduce-scatter.9.cloned.1.call-start = ((), (), s32[]{:S(2)}) async-start(), calls=%async_computation.8 | async-start | bytes 983040 | tf_op jit(solution)/shard_map/reduce_scatter | solution.py:70
  179.1 17.2 %copy-start.2 = (bf16[1280,768]{1,0:T(8,128)(2,1)S(1)}, bf16[1280,768]{1,0:T(8,128)(2,1)}, u32[]{:S(2)}) copy-start(bf16[1280,768]{1,0:T(8,128)(2,1)} %fusion.1) | copy-start | bytes 5898244
  196.3 27.2 %copy-start.3 = (f32[64,768]{1,0:T(8,128)S(1)}, f32[64,768]{1,0:T(8,128)}, u32[]{:S(2)}) copy-start(f32[64,768]{1,0:T(8,128)} %reduce-scatter.7.cloned.1.call-done) | copy-start | bytes 589828
  199.5 76.3 %reduce-scatter.11.cloned.1.call-start = ((), (), s32[]{:S(2)}) async-start(), calls=%async_computation.9 | async-start | bytes 1310720 | tf_op jit(solution)/shard_map/reduce_scatter | solution.py:86
  224.6 21.2 %copy-start.9 = (f32[256,1024]{1,0:T(8,128)S(1)}, f32[256,1024]{1,0:T(8,128)}, u32[]{:S(2)}) copy-start(f32[256,1024]{1,0:T(8,128)} %copy-done.8) | copy-start | bytes 3145732
Sparse Core Ops, SparseCore 0:
  9.5 51.8 all-gather.2
  63.4 48.8 all-gather.4
  115.7 22.9 reduce-scatter.4
  147.0 23.8 reduce-scatter.6
  199.6 23.8 reduce-scatter.8
  250.7 25.0 reduce-scatter.10
where the time goes:
time: 298 us; the launch traced here: 297 us
  waiting for transfers between devices  185 us (62%)
  blocking collectives  63.8 us (21%)
  matrix products  18.7 us (6%)
  between operations  14.3 us (5%)
  other arithmetic  13.1 us (4%)
    all_gather x1, waiting for transfers between devices, local(): w_down = lax.all_gather(down_weight, 'dp', axis=1, tiled=True)  48.5 us
    all_gather x1, waiting for transfers between devices, local(): w_up = lax.all_gather(up_weight, 'dp', axis=0, tiled=True)  44.1 us
    reduce_scatter x1, waiting for transfers between devices, local(): lax.psum_scatter(back_part, 'txt', scatter_dimension=0, tiled=True)  23.9 us
    reduce_scatter x1, waiting for transfers between devices, local(): lax.psum_scatter(normed_part, 'txt', scatter_dimension=1, tiled=True)  23.6 us
    reduce_scatter x1, waiting for transfers between devices, local(): mixed = lax.psum_scatter(mixed_part, 'txt', scatter_dimension=1, tiled=True)  22.2 us
    reduce_scatter x1, waiting for transfers between devices, local(): lax.psum_scatter(emb_part, 'txt', scatter_dimension=0, tiled=True)  21.7 us
    all_gather x1, blocking collectives, local(): gathered = lax.all_gather(resid, 'txt', axis=1, tiled=True)  8.89 us
    all_gather x1, blocking collectives, local(): lax.all_gather(output_gradient.astype(jnp.bfloat16), 'txt', axis=1, tiled...  6.85 us
  transfers between devices with their start and end apart: 6, of which 6 were waited for; matrix products, arithmetic and copies ran while one was open for 2% of the time, Pallas kernels for 0%

commit v1 on v0

--- a/solution.py
+++ b/solution.py
@@ -30,7 +30,9 @@
     input_inverse_deviation = lax.rsqrt(var_in + 1e-05)
     centered_input = (input_rows - input_mean) * input_inverse_deviation
     normed_input = (centered_input * prenorm_gain + prenorm_bias).astype(jnp.bfloat16)
-    w_up = lax.all_gather(up_weight, "dp", axis=0, tiled=True)
+    w_up = jnp.concatenate(
+        lax.all_to_all(jnp.stack([up_weight] * lax.axis_size("dp")), "dp", 0, 0), axis=0
+    )
     w_down = lax.all_gather(down_weight, "dp", axis=1, tiled=True)
     pre_act = jnp.dot(normed_input, w_up, preferred_element_type=jnp.float32) + up_bias
     gate_sig = jax.nn.sigmoid(1.702 * pre_act)

time: 298 us -> 283 us (0.950)
  waiting for transfers between devices: 185 us -> 161 us
  starting transfers between devices: 0.2 us -> 7.62 us
    all_to_all x0 -> x1, waiting for transfers between devices: none -> 55.8 us  [local(): lax.all_to_all(jnp.stack([up_weight] * lax.axis_size('dp')), 'dp', 0, 0)]
    all_gather x1 -> x0, waiting for transfers between devices: 44.1 us -> none  [local(): w_up = lax.all_gather(up_weight, 'dp', axis=0, tiled=True)]
    all_gather x1, waiting for transfers between devices: 48.5 us -> 11.4 us  [local(): w_down = lax.all_gather(down_weight, 'dp', axis=1, tiled=True)]
    all_to_all x0 -> x1, starting transfers between devices: none -> 7.42 us  [local(): lax.all_to_all(jnp.stack([up_weight] * lax.axis_size('dp')), 'dp', 0, 0)]
where the time goes in v1:
time: 283 us; the launch traced here: 282 us
  waiting for transfers between devices  161 us (57%)
  blocking collectives  62.6 us (22%)
  matrix products  18.8 us (7%)
  other arithmetic  14.7 us (5%)
  between operations  14 us (5%)
  starting transfers between devices  7.62 us (3%)
  local copies, waits for them, and re-layouts  3.58 us (1%)
    all_to_all x1, waiting for transfers between devices, local(): lax.all_to_all(jnp.stack([up_weight] * lax.axis_size('dp')), 'dp', 0, 0)  55.8 us
    reduce_scatter x1, waiting for transfers between devices, local(): lax.psum_scatter(normed_part, 'txt', scatter_dimension=1, tiled=True)  24.3 us
    reduce_scatter x1, waiting for transfers between devices, local(): lax.psum_scatter(back_part, 'txt', scatter_dimension=0, tiled=True)  23.9 us
    reduce_scatter x1, waiting for transfers between devices, local(): mixed = lax.psum_scatter(mixed_part, 'txt', scatter_dimension=1, tiled=True)  23.1 us
    reduce_scatter x1, waiting for transfers between devices, local(): lax.psum_scatter(emb_part, 'txt', scatter_dimension=0, tiled=True)  21.7 us
    all_gather x1, waiting for transfers between devices, local(): w_down = lax.all_gather(down_weight, 'dp', axis=1, tiled=True)  11.4 us
    all_to_all x1, starting transfers between devices, local(): lax.all_to_all(jnp.stack([up_weight] * lax.axis_size('dp')), 'dp', 0, 0)  7.42 us
    all_gather x1, blocking collectives, local(): lax.all_gather(output_gradient.astype(jnp.bfloat16), 'txt', axis=1, tiled...  7.29 us
  transfers between devices with their start and end apart: 6, of which 6 were waited for; matrix products, arithmetic and copies ran while one was open for 2% of the time, Pallas kernels for 0%

profile of v1, /device:TPU:0, one launch (start us, length us, event | category | flops | bytes accessed | tf_op | source)
XLA Modules:
  0.0 282.2 jit_solution(11454266367679624674)
XLA Ops:
  6.5 2.6 stack.2
  9.1 7.4 %all-to-all-start = ((bf16[8,128,1024]{2,1,0:T(8,128)(2,1)}), bf16[8,128,1024]{2,1,0:T(8,128)(2,1)S(1)}, u32[]{:S(2)}, u32[]{:S(2)}) async-start(bf16[8,128,1024]{2,1,0:T(8,128)(2,1)} %stack.2), calls=%async_computation | async-start | bytes 4194304 | tf_op jit(solution)/shard_map/all_to_all | solution.py:34
  17.3 7.2 %all_gather.15 = bf16[256,1024]{1,0:T(8,128)(2,1)S(1)} all-gather(bf16[256,256]{1,0:T(8,128)(2,1)S(1)} %copy-done.6), channel_id=1, replica_groups=mesh['dp'=8,'txt'=4] {'txt'}, dimensions={1}, use_global_device_ids=true | all-gather | bytes 655360 | tf_op jit(solution)/shard_map/all_gather | solution.py:26
  24.8 55.8 %all-to-all-done = bf16[8,128,1024]{2,1,0:T(8,128)(2,1)S(1)} async-done(((bf16[8,128,1024]{2,1,0:T(8,128)(2,1)}), bf16[8,128,1024]{2,1,0:T(8,128)(2,1)S(1)}, u32[]{:S(2)}, u32[]{:S(2)}) %all-to-all-start) | async-done | bytes 2097184 | tf_op jit(solution)/shard_map/all_to_all | solution.py:34
  80.6 1.8 convolution_add_fusion
  82.4 11.4 %all-gather.2.cloned.1.call-done = bf16[1024,1024]{1,0:T(8,128)(2,1)} async-done(((bf16[1024,128]{1,0:T(8,128)(2,1)}), bf16[1024,1024]{1,0:T(8,128)(2,1)}) %all-gather.2.cloned.1.call-update) | async-done | bytes 2097168 | tf_op jit(solution)/shard_map/all_gather | solution.py:36
  93.8 3.6 %fusion.17 = f32[256,1024]{1,0:T(8,128)} fusion(bf16[1024,1024]{1,0:T(8,128)(2,1)} %all-gather.2.cloned.1.call-done, f32[256,1024]{1,0:T(8,128)} %convolution_add_fusion), kind=kOutput, calls=%fused_computation.32 | convolution fusion | flops 538443776 | bytes 4194304 | tf_op jit(solution)/shard_map/dot_general | solution.py:40
  98.4 23.1 %reduce-scatter.5.cloned.1.call-done = f32[256,256]{1,0:T(8,128)} async-done(((f32[256,1024]{1,0:T(8,128)}), f32[256,256]{1,0:T(8,128)}) %reduce-scatter.5.cloned.1.call-update) | async-done | bytes 262160 | tf_op jit(solution)/shard_map/reduce_scatter | solution.py:41
  121.5 1.1 fusion.38
  122.6 5.8 %all-reduce.2 = (f32[256]{0:T(256)S(1)}, f32[256]{0:T(256)S(1)}) all-reduce(f32[256]{0:T(256)S(1)} %get-tuple-element.12, f32[256]{0:T(256)S(1)} %get-tuple-element.11), channel_id=1, replica_groups=mesh['dp'=8,'txt'=4] {'txt'}, use_global_device_ids=true, to_apply=%region_6.0 | all-reduce | flops 512 | bytes 4096 | tf_op jit(solution)/shard_map/psum | solution.py:44
  128.4 1.2 fusion.25
  130.2 1.7 fusion.1
  132.0 21.7 %reduce-scatter.7.cloned.1.call-done = f32[64,768]{1,0:T(8,128)} async-done(((f32[256,768]{1,0:T(8,128)}), f32[64,768]{1,0:T(8,128)}) %reduce-scatter.7.cloned.1.call-update) | async-done | bytes 196624 | tf_op jit(solution)/shard_map/reduce_scatter | solution.py:51
  153.7 1.0 multiply_reduce_fusion.6
  155.7 6.1 %all_gather.17 = bf16[256,768]{1,0:T(8,128)(2,1)S(1)} all-gather(bf16[64,768]{1,0:T(8,128)(2,1)S(1)} %fusion.35), channel_id=1, replica_groups=mesh['dp'=8,'txt'=4] {'txt'}, dimensions={0}, use_global_device_ids=true | all-gather | bytes 491520 | tf_op jit(solution)/shard_map/all_gather | solution.py:54
  161.9 3.5 %fusion.41 = (f32[256]{0:T(256)S(1)}, f32[256,1280]{1,0:T(8,128)}) fusion(bf16[256,768]{1,0:T(8,128)(2,1)S(1)} %all_gather.17, bf16[1280,768]{1,0:T(8,128)(2,1)} %fusion.1), kind=kOutput, calls=%fused_computation.81 | convolution fusion | flops 503971584 | bytes 3671040 | tf_op jit(solution)/shard_map/ie,je->ij/dot_general | solution.py:59
  165.4 6.4 %pmax.7 = f32[256]{0:T(256)S(1)} all-reduce(f32[256]{0:T(256)S(1)} %get-tuple-element.28), channel_id=1, replica_groups=mesh['dp'=8,'txt'=4] {'txt'}, use_global_device_ids=true, to_apply=%region_11.0 | all-reduce | flops 256 | bytes 2048 | tf_op jit(solution)/shard_map/pmax | solution.py:63
  171.8 1.6 fusion.3
  173.4 5.7 %psum.58 = f32[256]{0:T(256)S(1)} all-reduce(f32[256]{0:T(256)S(1)} %fusion.3), channel_id=1, replica_groups=mesh['dp'=8,'txt'=4] {'txt'}, use_global_device_ids=true, to_apply=%region_13.0 | all-reduce | flops 256 | bytes 2048 | tf_op jit(solution)/shard_map/psum | solution.py:65
  179.1 3.2 %fusion.12 = f32[256,768]{1,0:T(8,128)} fusion(bf16[1280,768]{1,0:T(8,128)(2,1)S(1)} %copy-done.2, f32[256,1280]{1,0:T(8,128)} %get-tuple-element.29, s32[256]{0:T(256)S(1)} %broadcast_subtract_fusion, f32[256]{0:T(256)S(1)} %psum.58, f32[256]{0:T(256)S(1)} %pmax.7), kind=kOutput, calls=%fused_computation.27 | convolution fusion | flops 505610240 | bytes 4066304 | tf_op jit(solution)/shard_map/dot_general | solution.py:71
  182.3 23.9 %reduce-scatter.9.cloned.1.call-done = f32[64,768]{1,0:T(8,128)} async-done(((f32[256,768]{1,0:T(8,128)}), f32[64,768]{1,0:T(8,128)}) %reduce-scatter.9.cloned.1.call-update) | async-done | bytes 196624 | tf_op jit(solution)/shard_map/reduce_scatter | solution.py:72
  206.3 1.1 multiply_reduce_fusion.5
  208.5 6.3 %all_gather.18 = bf16[256,768]{1,0:T(8,128)(2,1)S(1)} all-gather(bf16[64,768]{1,0:T(8,128)(2,1)S(1)} %divide_convert_fusion), channel_id=1, replica_groups=mesh['dp'=8,'txt'=4] {'txt'}, dimensions={0}, use_global_device_ids=true | all-gather | bytes 491520 | tf_op jit(solution)/shard_map/all_gather | solution.py:75
  215.8 6.4 %all-reduce.1 = (f32[256]{0:T(256)S(1)}, f32[256]{0:T(256)S(1)}) all-reduce(f32[256]{0:T(256)S(1)} %get-tuple-element.10, f32[256]{0:T(256)S(1)} %get-tuple-element.9), channel_id=1, replica_groups=mesh['dp'=8,'txt'=4] {'txt'}, use_global_device_ids=true, to_apply=%region_19.0 | all-reduce | flops 512 | bytes 4096 | tf_op jit(solution)/shard_map/psum | solution.py:78
  222.2 1.9 fusion.39
  224.0 7.3 %all_gather.19 = bf16[256,1024]{1,0:T(8,128)(2,1)} all-gather(bf16[256,256]{1,0:T(8,128)(2,1)S(1)} %get-tuple-element.21), channel_id=1, replica_groups=mesh['dp'=8,'txt'=4] {'txt'}, dimensions={1}, use_global_device_ids=true | all-gather | bytes 655360 | tf_op jit(solution)/shard_map/all_gather | solution.py:82
  231.3 4.5 %fusion.4 = f32[256,1024]{1,0:T(8,128)} fusion(bf16[1024,1024]{1,0:T(8,128)(2,1)S(1)} %bitcast.15, bf16[256,1024]{1,0:T(8,128)(2,1)} %all_gather.19, bf16[1024,1024]{1,0:T(8,128)(2,1)} %all-gather.2.cloned.1.call-done, f32[256,1024]{1,0:T(8,128)} %convolution_add_fusion), kind=kOutput, calls=%fused_computation.16 | convolution fusion | flops 1076363264 | bytes 6815744 | tf_op jit(solution)/shard_map/if,df->id/dot_general | solution.py:87
  236.8 24.3 %reduce-scatter.11.cloned.1.call-done = f32[256,256]{1,0:T(8,128)} async-done(((f32[256,1024]{1,0:T(8,128)}), f32[256,256]{1,0:T(8,128)}) %reduce-scatter.11.cloned.1.call-update) | async-done | bytes 262160 | tf_op jit(solution)/shard_map/reduce_scatter | solution.py:88
  261.1 1.1 multiply_reduce_fusion.4
  262.2 5.8 %all-reduce = (f32[256]{0:T(256)S(1)}, f32[256]{0:T(256)S(1)}) all-reduce(f32[256]{0:T(256)S(1)} %get-tuple-element.8, f32[256]{0:T(256)S(1)} %get-tuple-element.7), channel_id=1, replica_groups=mesh['dp'=8,'txt'=4] {'txt'}, use_global_device_ids=true, to_apply=%region_24.0 | all-reduce | flops 512 | bytes 4096 | tf_op jit(solution)/shard_map/psum | solution.py:95
  268.0 1.2 multiply_reduce_fusion
  269.2 5.7 %psum.63 = f32[256]{0:T(256)S(1)} all-reduce(f32[256]{0:T(256)S(1)} %get-tuple-element.19), channel_id=1, replica_groups=mesh['dp'=8,'txt'=4] {'txt'}, use_global_device_ids=true, to_apply=%region_26.0 | all-reduce | flops 256 | bytes 2048 | tf_op jit(solution)/shard_map/psum | solution.py:108
  (56 shorter events, 6.9 us)
Async XLA Ops:
  6.5 121.9 %copy-start = (bf16[256,768]{1,0:T(8,128)(2,1)S(1)}, bf16[256,768]{1,0:T(8,128)(2,1)}, u32[]{:S(2)}) copy-start(bf16[256,768]{1,0:T(8,128)(2,1)} %param.22) | copy-start | bytes 1179652
  9.1 8.2 %copy-start.6 = (bf16[256,256]{1,0:T(8,128)(2,1)S(1)}, bf16[256,256]{1,0:T(8,128)(2,1)}, u32[]{:S(2)}) copy-start(bf16[256,256]{1,0:T(8,128)(2,1)} %param.13) | copy-start | bytes 393220
  9.1 71.5 %copy-start.11 = (f32[1024]{0:T(1024)S(1)}, f32[1024]{0:T(1024)}, u32[]{:S(2)}) copy-start(f32[1024]{0:T(1024)} %param.14) | copy-start | bytes 12292
  9.1 71.5 %copy-start.12 = (f32[1024]{0:T(1024)S(1)}, f32[1024]{0:T(1024)}, u32[]{:S(2)}) copy-start(f32[1024]{0:T(1024)} %param.17) | copy-start | bytes 12292
  9.1 71.5 %copy-start.13 = (f32[1024]{0:T(1024)S(1)}, f32[1024]{0:T(1024)}, u32[]{:S(2)}) copy-start(f32[1024]{0:T(1024)} %param.15) | copy-start | bytes 12292
  9.1 71.5 %all-to-all-start = ((bf16[8,128,1024]{2,1,0:T(8,128)(2,1)}), bf16[8,128,1024]{2,1,0:T(8,128)(2,1)S(1)}, u32[]{:S(2)}, u32[]{:S(2)}) async-start(bf16[8,128,1024]{2,1,0:T(8,128)(2,1)} %stack.2), calls=%async_computation | async-start | bytes 4194304 | tf_op jit(solution)/shard_map/all_to_all | solution.py:34
  16.5 77.3 %all-gather.2.cloned.1.call-start = ((), (), s32[]{:S(2)}) async-start(), calls=%async_computation.5 | async-start | bytes 2359296 | tf_op jit(solution)/shard_map/all_gather | solution.py:36
  17.3 104.3 %reduce-scatter.5.cloned.1.call-start = ((), (), s32[]{:S(2)}) async-start(), calls=%async_computation.6 | async-start | bytes 1310720 | tf_op jit(solution)/shard_map/reduce_scatter | solution.py:41
  80.6 1.8 copy-start.4
  82.4 46.0 %copy-start.8 = (f32[256]{0:T(256)S(1)}, f32[256]{0:T(256)}, u32[]{:S(2)}) copy-start(f32[256]{0:T(256)} %param.20) | copy-start | bytes 3076
  82.4 46.0 %copy-start.10 = (f32[256]{0:T(256)S(1)}, f32[256]{0:T(256)}, u32[]{:S(2)}) copy-start(f32[256]{0:T(256)} %param.21) | copy-start | bytes 3076
  97.4 32.3 %copy-start.9 = (s32[256]{0:T(256)S(1)}, s32[256]{0:T(256)}, u32[]{:S(2)}) copy-start(s32[256]{0:T(256)} %param.24) | copy-start | bytes 3076
  97.4 32.3 %copy-start.1 = (bf16[1280,768]{1,0:T(8,128)(2,1)S(1)}, bf16[1280,768]{1,0:T(8,128)(2,1)}, u32[]{:S(2)}) copy-start(bf16[1280,768]{1,0:T(8,128)(2,1)} %param.23) | copy-start | bytes 5898244
  97.5 56.2 %reduce-scatter.7.cloned.1.call-start = ((), (), s32[]{:S(2)}) async-start(), calls=%async_computation.7 | async-start | bytes 983040 | tf_op jit(solution)/shard_map/reduce_scatter | solution.py:51
  129.7 76.6 %reduce-scatter.9.cloned.1.call-start = ((), (), s32[]{:S(2)}) async-start(), calls=%async_computation.8 | async-start | bytes 983040 | tf_op jit(solution)/shard_map/reduce_scatter | solution.py:72
  161.9 17.2 %copy-start.2 = (bf16[1280,768]{1,0:T(8,128)(2,1)S(1)}, bf16[1280,768]{1,0:T(8,128)(2,1)}, u32[]{:S(2)}) copy-start(bf16[1280,768]{1,0:T(8,128)(2,1)} %fusion.1) | copy-start | bytes 5898244
  179.1 27.2 %copy-start.3 = (f32[64,768]{1,0:T(8,128)S(1)}, f32[64,768]{1,0:T(8,128)}, u32[]{:S(2)}) copy-start(f32[64,768]{1,0:T(8,128)} %reduce-scatter.7.cloned.1.call-done) | copy-start | bytes 589828
  182.3 78.8 %reduce-scatter.11.cloned.1.call-start = ((), (), s32[]{:S(2)}) async-start(), calls=%async_computation.9 | async-start | bytes 1310720 | tf_op jit(solution)/shard_map/reduce_scatter | solution.py:88
  208.4 22.9 %copy-start.5 = (bf16[8,128,1024]{2,1,0:T(8,128)(2,1)S(1)}, bf16[8,128,1024]{2,1,0:T(8,128)(2,1)}, u32[]{:S(2)}) copy-start(bf16[8,128,1024]{2,1,0:T(8,128)(2,1)} %copy-done.4) | copy-start | bytes 6291460
  235.8 32.1 %copy-start.7 = (f32[256,256]{1,0:T(8,128)S(1)}, f32[256,256]{1,0:T(8,128)}, u32[]{:S(2)}) copy-start(f32[256,256]{1,0:T(8,128)} %get-tuple-element.22) | copy-start | bytes 786436
Sparse Core Ops, SparseCore 0:
  19.4 74.3 all-gather.1
  97.6 23.9 reduce-scatter.4
  129.8 23.8 reduce-scatter.6
  182.4 23.8 reduce-scatter.8
  236.0 25.0 reduce-scatter.10
